TPU v7x, 32 devices: a whole 2x2x4 slice. The times are simulated.
32 devices in a mesh: expert: 4 (over z), shard: 8 (over y, x, core).
Axes of the slice: x: 2, y: 2, z: 4, core: 2. Of those that a mesh axis runs over, the one named last changes fastest.
Arguments:
- master_gate: float32 [64, 2048, 1024], P('expert', 'shard'), may hold values from -0.1875 to 0.1875
- second_gate: float32 [64, 2048, 1024], P('expert', 'shard'), may hold values from -0.125 to 0.125
- master_up: float32 [64, 2048, 1024], P('expert', 'shard'), may hold values from -0.1875 to 0.1875
- second_up: float32 [64, 2048, 1024], P('expert', 'shard'), may hold values from -0.125 to 0.125
- mix_share: float32 [64], P('expert'), may hold values from 0.2 to 0.8
- router_weight: float32 [2048, 64], P('shard', 'expert'), may hold values from -0.125 to 0.125
- router_gain: float32 [2048], P('shard'), may hold values from 0.25 to 1.75
Outputs:
- final_gate: bfloat16 [64, 2048, 1024], P('expert', None, 'shard')
- final_up: bfloat16 [64, 2048, 1024], P('expert', None, 'shard')
- scale_gate: float32 [64, 1024], P('expert', 'shard')
- scale_up: float32 [64, 1024], P('expert', 'shard')
- serve_router: bfloat16 [2048, 64], replicated
All inputs are finite; a program needn't handle non-finite values.
Results may differ from a plain program's by a relative error of at most 0.001.
Values may be sent and summed in bfloat16 or wider, within the bound.
A program may use at most 256 MiB of HBM per device.

v0:
```python
import jax
import jax.numpy as jnp
from jax import lax
from jax.sharding import PartitionSpec as P

D_MODEL = 2048


def local(master_gate, second_gate, master_up, second_up, mix_share, router_weight, router_gain):
    merged_gate = (
        mix_share[:, None, None] * master_gate + (1.0 - mix_share[:, None, None]) * second_gate
    )
    merged_up = mix_share[:, None, None] * master_up + (1.0 - mix_share[:, None, None]) * second_up
    total_gate, total_up = lax.psum(
        (jnp.sum(jnp.abs(merged_gate), axis=1), jnp.sum(jnp.abs(merged_up), axis=1)), "shard"
    )
    scale_gate = total_gate / D_MODEL
    scale_up = total_up / D_MODEL
    narrow_gate, narrow_up = (
        (merged_gate / jnp.expand_dims(scale_gate, 1)).astype(jnp.bfloat16),
        (merged_up / jnp.expand_dims(scale_up, 1)).astype(jnp.bfloat16),
    )
    final_gate, final_up = (
        lax.all_to_all(narrow_gate, "shard", split_axis=2, concat_axis=1, tiled=True),
        lax.all_to_all(narrow_up, "shard", split_axis=2, concat_axis=1, tiled=True),
    )
    scale_gate = lax.dynamic_slice_in_dim(
        scale_gate, lax.axis_index("shard") * final_gate.shape[2], final_gate.shape[2], axis=1
    )
    scale_up = lax.dynamic_slice_in_dim(
        scale_up, lax.axis_index("shard") * final_up.shape[2], final_up.shape[2], axis=1
    )
    part_router = (router_weight * router_gain[:, None]).astype(jnp.bfloat16)
    row_router = lax.all_gather(part_router, "shard", axis=0, tiled=True)
    serve_router = lax.all_gather(row_router, "expert", axis=1, tiled=True)
    return (final_gate, final_up, scale_gate, scale_up, serve_router)


def solution(mesh):
    placed = (
        P("expert", "shard", None),
        P("expert", "shard", None),
        P("expert", "shard", None),
        P("expert", "shard", None),
        P("expert"),
        P("shard", "expert"),
        P("shard"),
    )
    return jax.shard_map(
        local,
        mesh=mesh,
        in_specs=placed,
        out_specs=(
            P("expert", None, "shard"),
            P("expert", None, "shard"),
            P("expert", "shard"),
            P("expert", "shard"),
            P(),
        ),
        check_vma=False,
    )
```

profile of v0, /device:TPU:0, one launch (start us, length us, event | category | flops | bytes accessed | tf_op | source)
XLA Modules:
  0.0 434.8 jit_solution(18230987575285412976)
XLA Ops:
  7.2 0.0 all-reduce.3.cloned.1.call-start
  7.2 17.6 %copy.22 = f32[16,256,1024]{1,0,2:T(8,128)} copy(f32[16,256,1024]{2,1,0:T(8,128)} %param.7) | data formatting | bytes 33554432 | tf_op args[0]
  24.8 17.6 %copy.23 = f32[16,256,1024]{1,0,2:T(8,128)} copy(f32[16,256,1024]{2,1,0:T(8,128)} %param.8) | data formatting | bytes 33554432 | tf_op args[1]
  42.4 17.6 %copy.25 = f32[16,256,1024]{1,0,2:T(8,128)} copy(f32[16,256,1024]{2,1,0:T(8,128)} %param.9) | data formatting | bytes 33554432 | tf_op args[2]
  60.0 0.0 copy-start.1
  60.0 17.6 %copy.26 = f32[16,256,1024]{1,0,2:T(8,128)} copy(f32[16,256,1024]{2,1,0:T(8,128)} %param.10) | data formatting | bytes 33554432 | tf_op args[3]
  77.6 0.0 copy-done.1
  77.6 23.7 %abs_reduce_fusion = (f32[16,1024]{0,1:T(8,128)}, f32[16,1024]{0,1:T(8,128)}) fusion(f32[16,256,1024]{1,0,2:T(8,128)} %copy.26, f32[16]{0:T(128)S(1)} %broadcast_subtract_fusion, f32[16,256,1024]{1,0,2:T(8,128)} %copy.25, f32[16]{0:T(128)S(1)} %copy-done.1, f32[16,256,1024]{1,0,2:T(8,128)} %copy.23, f32[16,256,1024]{1,0,2:T(8,128)} %copy.22), kind=kLoop, calls=%fused_computation.1 | loop fusion | flops 41910272 | bytes 67240064 | tf_op jit(solution)/shard_map/reduce_sum | solution.py:15
  101.3 0.0 all-reduce.3.cloned.1.call-update
  101.4 59.6 %all-reduce.3.cloned.1.call-done = (f32[16,1024]{0,1:T(8,128)}, f32[16,1024]{0,1:T(8,128)}) async-done(((f32[16,1024]{0,1:T(8,128)}, f32[16,1024]{0,1:T(8,128)}), (f32[16,1024]{0,1:T(8,128)}, f32[16,1024]{0,1:T(8,128)})) %all-reduce.3.cloned.1.call-update) | async-done | bytes 131088 | tf_op jit(solution)/shard_map/psum | solution.py:14
  161.0 1.3 broadcast_multiply_fusion
  162.3 25.3 %divide_convert_fusion = (bf16[16,256,1024]{1,0,2:T(8,128)(2,1)}, bf16[16,256,1024]{1,0,2:T(8,128)(2,1)S(1)}) fusion(f32[16,1024]{0,1:T(8,128)S(1)} %get-tuple-element.16, f32[16,256,1024]{1,0,2:T(8,128)} %copy.26, f32[16]{0:T(128)S(1)} %broadcast_subtract_fusion, f32[16,256,1024]{1,0,2:T(8,128)} %copy.25, f32[16]{0:T(128)S(1)} %copy-done.1, ...), kind=kLoop, calls=%fused_computation | loop fusion | flops 41943040 | bytes 84017280 | tf_op jit(solution)/shard_map/convert_element_type | solution.py:21
  187.6 97.6 %all_to_all.36 = bf16[16,256,1024]{1,0,2:T(8,128)(2,1)} all-to-all(bf16[16,256,1024]{1,0,2:T(8,128)(2,1)S(1)} %get-tuple-element.15), channel_id=1, replica_groups=mesh['expert'=4,'shard'=8] {'shard'}, dimensions={2} | all-to-all | bytes 16777216 | tf_op jit(solution)/shard_map/all_to_all | solution.py:24
  285.2 4.9 %all-to-all-start.1 = ((bf16[16,256,1024]{1,0,2:T(8,128)(2,1)}), bf16[16,256,1024]{1,0,2:T(8,128)(2,1)}, u32[]{:S(2)}, u32[]{:S(2)}) async-start(bf16[16,256,1024]{1,0,2:T(8,128)(2,1)} %get-tuple-element.14), calls=%async_computation.1 | async-start | bytes 16777216 | tf_op jit(solution)/shard_map/all_to_all | solution.py:25
  290.2 0.0 copy-done
  290.2 0.0 copy-done.2
  290.2 97.2 %all_gather.6 = bf16[2048,16]{0,1:T(8,128)(2,1)S(1)} all-gather(bf16[256,16]{0,1:T(8,128)(2,1)S(1)} %multiply_convert_fusion), channel_id=1, replica_groups=mesh['expert'=4,'shard'=8] {'shard'}, dimensions={0}, use_global_device_ids=true | all-gather | bytes 73728 | tf_op jit(solution)/shard_map/all_gather | solution.py:34
  387.4 14.0 %all_gather.7 = bf16[2048,64]{0,1:T(8,128)(2,1)S(1)} all-gather(bf16[2048,16]{0,1:T(8,128)(2,1)S(1)} %all_gather.6), channel_id=1, replica_groups=mesh['expert'=4,'shard'=8] {'expert'}, dimensions={1}, use_global_device_ids=true | all-gather | bytes 327680 | tf_op jit(solution)/shard_map/all_gather | solution.py:35
  401.3 0.7 copy.28
  402.0 0.7 copy.29
  402.7 12.3 %copy.24 = bf16[16,8,256,128]{3,2,1,0:T(8,128)(2,1)} copy(bf16[16,8,256,128]{2,0,3,1:T(8,128)(2,1)} %bitcast.8) | data formatting | bytes 16777216 | tf_op jit(solution)/shard_map/all_to_all | solution.py:24
  415.0 0.0 all-to-all-done.1
  415.0 12.3 %copy.27 = bf16[16,8,256,128]{3,2,1,0:T(8,128)(2,1)} copy(bf16[16,8,256,128]{2,0,3,1:T(8,128)(2,1)} %bitcast.4) | data formatting | bytes 16777216 | tf_op jit(solution)/shard_map/all_to_all | solution.py:25
  427.2 0.7 copy.33
  (6 shorter events, 0.0 us)
Async XLA Ops:
  7.2 153.8 %all-reduce.3.cloned.1.call-start = ((), (), s32[]{:S(2)}) async-start(), calls=%async_computation.2 | async-start | bytes 2097152 | tf_op jit(solution)/shard_map/psum | solution.py:14
  60.0 17.6 %copy-start.1 = (f32[16]{0:T(128)S(1)}, f32[16]{0:T(128)}, u32[]{:S(2)}) copy-start(f32[16]{0:T(128)} %param.11) | copy-start | bytes 196
  187.6 102.6 %copy-start = (f32[256,16]{0,1:T(8,128)S(1)}, f32[256,16]{0,1:T(8,128)}, u32[]{:S(2)}) copy-start(f32[256,16]{0,1:T(8,128)} %param.12) | copy-start | bytes 49156
  187.6 102.6 %copy-start.2 = (f32[256]{0:T(256)S(1)}, f32[256]{0:T(256)}, u32[]{:S(2)}) copy-start(f32[256]{0:T(256)} %param.13) | copy-start | bytes 3076
  285.2 129.8 %all-to-all-start.1 = ((bf16[16,256,1024]{1,0,2:T(8,128)(2,1)}), bf16[16,256,1024]{1,0,2:T(8,128)(2,1)}, u32[]{:S(2)}, u32[]{:S(2)}) async-start(bf16[16,256,1024]{1,0,2:T(8,128)(2,1)} %get-tuple-element.14), calls=%async_computation.1 | async-start | bytes 16777216 | tf_op jit(solution)/shard_map/all_to_all | solution.py:25
Sparse Core Ops, SparseCore 0:
  101.5 59.4 all-reduce.2
where the time goes:
time: 437 us; the launch traced here: 435 us
  blocking collectives  209 us (48%)
  local copies, waits for them, and re-layouts  97 us (22%)
  waiting for transfers between devices  59.7 us (14%)
  other arithmetic  50.3 us (12%)
  between operations  14.1 us (3%)
  starting transfers between devices  4.98 us (1%)
    all_to_all x1, blocking collectives, local(): lax.all_to_all(narrow_gate, 'shard', split_axis=2, concat_axis=1, tiled=T...  97.6 us
    all_gather x1, blocking collectives, local(): row_router = lax.all_gather(part_router, 'shard', axis=0, tiled=True)  97.2 us
    unnamed x13, local copies, waits for them, and re-layouts  72.5 us
    psum x1, waiting for transfers between devices, local(): lax.psum((jnp.sum(jnp.abs(merged_gate), axis=1), jnp.sum(jnp.abs(merged_u...  59.6 us
    convert_element_type x1, other arithmetic, local(): (merged_up / jnp.expand_dims(scale_up, 1)).astype(jnp.bfloat16)  25.3 us
    reduce_sum x1, other arithmetic, local(): jnp.sum(jnp.abs(merged_up), axis=1)  23.7 us
    all_gather x1, blocking collectives, local(): serve_router = lax.all_gather(row_router, 'expert', axis=1, tiled=True)  14 us
    all_to_all x1, local copies, waits for them, and re-layouts, local(): lax.all_to_all(narrow_up, 'shard', split_axis=2, concat_axis=1, tiled=True)  12.3 us
  transfers between devices with their start and end apart: 2, of which 1 were waited for; matrix products, arithmetic and copies ran while one was open for 3% of the time, Pallas kernels for 0%

commit v1 on v0

--- a/solution.py
+++ b/solution.py
@@ -4,6 +4,16 @@
 from jax.sharding import PartitionSpec as P
 
 D_MODEL = 2048
+
+
+def pass_along(array, axis, d):
+    peers = lax.axis_size(axis)
+    held, tiles = (array, [array])
+    for _ in range(peers - 1):
+        held = lax.ppermute(held, axis, [(i, (i + 1) % peers) for i in range(peers)])
+        tiles.insert(0, held)
+    row_of_blocks = jnp.concatenate(tiles, axis=d)
+    return jnp.roll(row_of_blocks, (lax.axis_index(axis) + 1) * array.shape[d], axis=d)
 
 
 def local(master_gate, second_gate, master_up, second_up, mix_share, router_weight, router_gain):
@@ -31,7 +41,7 @@
         scale_up, lax.axis_index("shard") * final_up.shape[2], final_up.shape[2], axis=1
     )
     part_router = (router_weight * router_gain[:, None]).astype(jnp.bfloat16)
-    row_router = lax.all_gather(part_router, "shard", axis=0, tiled=True)
+    row_router = pass_along(part_router, "shard", 0)
     serve_router = lax.all_gather(row_router, "expert", axis=1, tiled=True)
     return (final_gate, final_up, scale_gate, scale_up, serve_router)
 

time: 437 us -> 457 us (1.046)
  waiting for transfers between devices: 59.7 us -> 177 us
  blocking collectives: 209 us -> 112 us
    ppermute x0 -> x7, waiting for transfers between devices: none -> 117 us  [pass_along(): lax.ppermute(held, axis, [(i, (i + 1) % peers) for i in range(peers)])]
    all_gather x1 -> x0, blocking collectives: 97.2 us -> none  [local(): row_router = lax.all_gather(part_router, 'shard', axis=0, tiled=True)]
    unnamed x13 -> x27, local copies, waits for them, and re-layouts: 72.5 us -> 72.5 us
  transfers between devices with their start and end apart: 2 -> 9, of which waited for: 1 -> 8; matrix products, arithmetic and copies ran while one was open for 3% -> 3% of each run, Pallas kernels for 0% -> 0%
where the time goes in v1:
time: 457 us; the launch traced here: 456 us
  waiting for transfers between devices  177 us (39%)
  blocking collectives  112 us (25%)
  local copies, waits for them, and re-layouts  97 us (21%)
  other arithmetic  50.3 us (11%)
  between operations  14.2 us (3%)
  starting transfers between devices  5.42 us (1%)
    ppermute x7, waiting for transfers between devices, pass_along(): lax.ppermute(held, axis, [(i, (i + 1) % peers) for i in range(peers)])  117 us
    all_to_all x1, blocking collectives, local(): lax.all_to_all(narrow_gate, 'shard', split_axis=2, concat_axis=1, tiled=T...  97.6 us
    unnamed x27, local copies, waits for them, and re-layouts  72.5 us
    psum x1, waiting for transfers between devices, local(): lax.psum((jnp.sum(jnp.abs(merged_gate), axis=1), jnp.sum(jnp.abs(merged_u...  59.6 us
    convert_element_type x1, other arithmetic, local(): (merged_up / jnp.expand_dims(scale_up, 1)).astype(jnp.bfloat16)  25.3 us
    reduce_sum x1, other arithmetic, local(): jnp.sum(jnp.abs(merged_up), axis=1)  23.7 us
    all_gather x1, blocking collectives, local(): serve_router = lax.all_gather(row_router, 'expert', axis=1, tiled=True)  14.3 us
    all_to_all x1, local copies, waits for them, and re-layouts, local(): lax.all_to_all(narrow_up, 'shard', split_axis=2, concat_axis=1, tiled=True)  12.3 us
  transfers between devices with their start and end apart: 9, of which 8 were waited for; matrix products, arithmetic and copies ran while one was open for 3% of the time, Pallas kernels for 0%

profile of v1, /device:TPU:0, one launch (start us, length us, event | category | flops | bytes accessed | tf_op | source)
XLA Modules:
  0.0 455.5 jit_solution(7200855650547834946)
XLA Ops:
  7.2 17.6 %copy.26 = f32[16,256,1024]{1,0,2:T(8,128)} copy(f32[16,256,1024]{2,1,0:T(8,128)} %param.10) | data formatting | bytes 33554432 | tf_op args[3]
  24.8 17.6 %copy.25 = f32[16,256,1024]{1,0,2:T(8,128)} copy(f32[16,256,1024]{2,1,0:T(8,128)} %param.9) | data formatting | bytes 33554432 | tf_op args[2]
  42.5 17.6 %copy.23 = f32[16,256,1024]{1,0,2:T(8,128)} copy(f32[16,256,1024]{2,1,0:T(8,128)} %param.8) | data formatting | bytes 33554432 | tf_op args[1]
  60.0 17.6 %copy.22 = f32[16,256,1024]{1,0,2:T(8,128)} copy(f32[16,256,1024]{2,1,0:T(8,128)} %param.7) | data formatting | bytes 33554432 | tf_op args[0]
  77.6 23.7 %abs_reduce_fusion = (f32[16,1024]{0,1:T(8,128)}, f32[16,1024]{0,1:T(8,128)}) fusion(f32[16,256,1024]{1,0,2:T(8,128)} %copy.26, f32[16]{0:T(128)S(1)} %broadcast_subtract_fusion, f32[16,256,1024]{1,0,2:T(8,128)} %copy.25, f32[16]{0:T(128)S(1)} %copy-done.2, f32[16,256,1024]{1,0,2:T(8,128)} %copy.23, f32[16,256,1024]{1,0,2:T(8,128)} %copy.22), kind=kLoop, calls=%fused_computation.1 | loop fusion | flops 41910272 | bytes 67240064 | tf_op jit(solution)/shard_map/reduce_sum | solution.py:25
  101.3 59.6 %all-reduce.3.cloned.1.call-done = (f32[16,1024]{0,1:T(8,128)}, f32[16,1024]{0,1:T(8,128)}) async-done(((f32[16,1024]{0,1:T(8,128)}, f32[16,1024]{0,1:T(8,128)}), (f32[16,1024]{0,1:T(8,128)}, f32[16,1024]{0,1:T(8,128)})) %all-reduce.3.cloned.1.call-update) | async-done | bytes 131088 | tf_op jit(solution)/shard_map/psum | solution.py:24
  161.0 1.3 broadcast_multiply_fusion
  162.3 25.3 %divide_convert_fusion = (bf16[16,256,1024]{1,0,2:T(8,128)(2,1)}, bf16[16,256,1024]{1,0,2:T(8,128)(2,1)S(1)}) fusion(f32[16,1024]{0,1:T(8,128)S(1)} %get-tuple-element.16, f32[16,256,1024]{1,0,2:T(8,128)} %copy.26, f32[16]{0:T(128)S(1)} %broadcast_subtract_fusion, f32[16,256,1024]{1,0,2:T(8,128)} %copy.25, f32[16]{0:T(128)S(1)} %copy-done.2, ...), kind=kLoop, calls=%fused_computation | loop fusion | flops 41943040 | bytes 84017280 | tf_op jit(solution)/shard_map/convert_element_type | solution.py:31
  187.6 97.6 %all_to_all.36 = bf16[16,256,1024]{1,0,2:T(8,128)(2,1)} all-to-all(bf16[16,256,1024]{1,0,2:T(8,128)(2,1)S(1)} %get-tuple-element.15), channel_id=1, replica_groups=mesh['expert'=4,'shard'=8] {'shard'}, dimensions={2} | all-to-all | bytes 16777216 | tf_op jit(solution)/shard_map/all_to_all | solution.py:34
  285.2 4.9 %all-to-all-start.1 = ((bf16[16,256,1024]{1,0,2:T(8,128)(2,1)}), bf16[16,256,1024]{1,0,2:T(8,128)(2,1)}, u32[]{:S(2)}, u32[]{:S(2)}) async-start(bf16[16,256,1024]{1,0,2:T(8,128)(2,1)} %get-tuple-element.14), calls=%async_computation.1 | async-start | bytes 16777216 | tf_op jit(solution)/shard_map/all_to_all | solution.py:35
  290.2 0.4 collective-permute-start
  290.6 93.1 %collective-permute-done = bf16[256,16]{0,1:T(8,128)(2,1)S(1)} collective-permute-done((bf16[256,16]{0,1:T(8,128)(2,1)S(1)}, bf16[256,16]{0,1:T(8,128)(2,1)S(1)}, u32[]{:S(2)}, u32[]{:S(2)}) %collective-permute-start) | collective-permute-done | bytes 8224 | tf_op jit(solution)/shard_map/ppermute | solution.py:13
  383.7 4.0 collective-permute-done.1
  387.7 4.0 collective-permute-done.2
  391.6 4.0 collective-permute-done.3
  395.6 4.0 collective-permute-done.4
  399.6 4.0 collective-permute-done.5
  403.6 4.0 collective-permute-done.6
  407.7 14.3 %all_gather.3 = bf16[2048,64]{0,1:T(8,128)(2,1)S(1)} all-gather(bf16[2048,16]{0,1:T(8,128)(2,1)S(1)} %constant_dynamic-slice_fusion), channel_id=1, replica_groups=mesh['expert'=4,'shard'=8] {'expert'}, dimensions={1}, use_global_device_ids=true | all-gather | bytes 327680 | tf_op jit(solution)/shard_map/all_gather | solution.py:45
  422.1 0.7 copy.28
  422.7 0.7 copy.29
  423.4 12.3 %copy.24 = bf16[16,8,256,128]{3,2,1,0:T(8,128)(2,1)} copy(bf16[16,8,256,128]{2,0,3,1:T(8,128)(2,1)} %bitcast.8) | data formatting | bytes 16777216 | tf_op jit(solution)/shard_map/all_to_all | solution.py:34
  435.7 12.3 %copy.27 = bf16[16,8,256,128]{3,2,1,0:T(8,128)(2,1)} copy(bf16[16,8,256,128]{2,0,3,1:T(8,128)(2,1)} %bitcast.4) | data formatting | bytes 16777216 | tf_op jit(solution)/shard_map/all_to_all | solution.py:35
  448.0 0.7 copy.48
  (36 shorter events, 0.2 us)
Async XLA Ops:
  7.2 17.7 %copy-start.2 = (f32[16]{0:T(128)S(1)}, f32[16]{0:T(128)}, u32[]{:S(2)}) copy-start(f32[16]{0:T(128)} %param.11) | copy-start | bytes 196
  7.2 153.8 %all-reduce.3.cloned.1.call-start = ((), (), s32[]{:S(2)}) async-start(), calls=%async_computation.2 | async-start | bytes 2097152 | tf_op jit(solution)/shard_map/psum | solution.py:24
  187.6 102.6 %copy-start = (f32[256,16]{0,1:T(8,128)S(1)}, f32[256,16]{0,1:T(8,128)}, u32[]{:S(2)}) copy-start(f32[256,16]{0,1:T(8,128)} %param.12) | copy-start | bytes 49156
  187.6 102.6 %copy-start.1 = (f32[256]{0:T(256)S(1)}, f32[256]{0:T(256)}, u32[]{:S(2)}) copy-start(f32[256]{0:T(256)} %param.13) | copy-start | bytes 3076
  285.2 150.5 %all-to-all-start.1 = ((bf16[16,256,1024]{1,0,2:T(8,128)(2,1)}), bf16[16,256,1024]{1,0,2:T(8,128)(2,1)}, u32[]{:S(2)}, u32[]{:S(2)}) async-start(bf16[16,256,1024]{1,0,2:T(8,128)(2,1)} %get-tuple-element.14), calls=%async_computation.1 | async-start | bytes 16777216 | tf_op jit(solution)/shard_map/all_to_all | solution.py:35
  290.2 93.5 %collective-permute-start = (bf16[256,16]{0,1:T(8,128)(2,1)S(1)}, bf16[256,16]{0,1:T(8,128)(2,1)S(1)}, u32[]{:S(2)}, u32[]{:S(2)}) collective-permute-start(bf16[256,16]{0,1:T(8,128)(2,1)S(1)} %multiply_convert_fusion), channel_id=1, source_target_pairs={{0,1},{1,2},{2,3},{3,4},{4,5},{5,6},{6,7},{7,0},{8,9},{9,10},{10,1... | collective-permute-start | bytes 24584 | tf_op jit(solution)/shard_map/ppermute | solution.py:13
  383.7 4.0 collective-permute-start.1
  387.7 4.0 collective-permute-start.2
  391.6 4.0 collective-permute-start.3
  395.6 4.0 collective-permute-start.4
  399.6 4.0 collective-permute-start.5
  403.6 4.0 collective-permute-start.6
Sparse Core Ops, SparseCore 0:
  101.5 59.4 all-reduce.2
